TPU v7x, 128 devices: a 2x2x16 block of a 8x8x16 slice. The times are simulated.
128 devices in a mesh: groups: 4 (over x, y), samp: 32 (over z, core).
Axes of the slice: x: 2, y: 2, z: 16, core: 2. Of those that a mesh axis runs over, the one named last changes fastest.
The devices are a block of a 8x8x16 slice.
Arguments:
- dosage: bfloat16 [32768, 8192], P(('groups', 'samp')), parts along dimension 0, may hold values from 0 to 2
- covariates: bfloat16 [32768, 96], P(('groups', 'samp')), parts along dimension 0, may hold values from -8 to 8
- expression: bfloat16 [32768, 16384], P('groups', 'samp'), parts along dimension 0, may hold values from -10 to 10
- block_index: int32 [8, 1024], P('groups'), parts along dimension 0, may hold values from 0 to 8191
- expr_row: int32 [32768], P('groups'), parts along dimension 0, may hold values from 0 to 8191, each once
Outputs:
- zscore: float32 [8192, 16384], P('groups', 'samp'), parts along dimension 0
There are 4 independent parts, one for each index of `groups`. A program takes and returns all parts, laid end to end along the dimension named above; each array names one. Nothing has to cross between parts.
Inputs may be any that keep to these rules, and one draw needn't show every extreme that they name: `expr_row`: every expression row appears once.
All inputs are finite; a program needn't handle non-finite values.
Results may differ from a plain program's by a relative error of at most 0.0029.
Values may be sent and summed in bfloat16 or wider, within the bound.
A program may use at most 192 MiB of HBM per device.

v0:
```python
import math

import jax
import jax.numpy as jnp
from jax import lax
from jax.experimental import pallas as pl
from jax.experimental.pallas import tpu as pltpu
from jax.sharding import PartitionSpec as P

MESH = pl.DeviceIdType.MESH
HIGHEST = lax.Precision.HIGHEST
F32 = jnp.float32
BF16 = jnp.bfloat16
epsilon = 1e-06
CHUNKS = 8
PARTS = 4


def dot(a, b, contract, precision=None):
    return lax.dot_general(
        a, b, ((contract[:1], contract[1:]), ((), ())), precision=precision, preferred_element_type=F32
    )


def scan_kernel(
    scale, length,
    d_hbm, e_hbm, xt_ref, pick_ref, perm_ref,
    out_hbm, pn_ref,
    a, xt, e, m, d, acc, lac, sq, pacc, kacc, gram, xtm, h,
    ring_send, ring_recv, sib_send, sib_recv, x_send, x_recv, xs_send, xs_recv, load_sem, out_sem,
):
    half = length // 2
    last = half // 2
    end = half - 1
    me = lax.axis_index("samp")
    z = lax.div(me, 2)
    core = lax.rem(me, 2)
    up = lax.rem(me + 2, length)
    down = lax.rem(me + length - 2, length)
    sib = me + 1 - 2 * core
    chunk = a.shape[1] // CHUNKS
    rows = a.shape[2]
    covars = xt.shape[1]
    panel = d.shape[1] // PARTS
    order = e.shape[0] // PARTS

    def place(n):
        s = lax.div(n + 1, 2)
        sign = 2 * lax.rem(n + 1, 2) - 1
        return lax.rem(z + sign * s + half, half)

    def block(q, b):
        return a.at[b, pl.ds(pl.multiple_of(q * chunk, chunk), chunk), :]

    def ring(q, n, target, index, arrival):
        ref = block(q, 2 * place(n) + core)
        return pltpu.make_async_remote_copy(
            src_ref=ref, dst_ref=ref, send_sem=ring_send.at[q, index], recv_sem=ring_recv.at[q, arrival],
            device_id={"samp": target}, device_id_type=MESH,
        )

    def across(q, n):
        ref = block(q, 2 * place(n) + core)
        return pltpu.make_async_remote_copy(
            src_ref=ref, dst_ref=ref, send_sem=sib_send.at[q, n], recv_sem=sib_recv.at[q, n],
            device_id={"samp": sib}, device_id_type=MESH,
        )

    def x_ring(n, target, index, arrival):
        ref = xt.at[2 * place(n) + core]
        return pltpu.make_async_remote_copy(
            src_ref=ref, dst_ref=ref, send_sem=x_send.at[index], recv_sem=x_recv.at[arrival],
            device_id={"samp": target}, device_id_type=MESH,
        )

    def x_across(n):
        ref = xt.at[2 * place(n) + core]
        return pltpu.make_async_remote_copy(
            src_ref=ref, dst_ref=ref, send_sem=xs_send.at[n], recv_sem=xs_recv.at[n],
            device_id={"samp": sib}, device_id_type=MESH,
        )

    def own(q):
        return (ring(q, 0, up, 0, 1), ring(q, 0, down, half, 2), across(q, 0))

    def comm(q, s, parity, link, cross, finish):
        def arrive(n, target, forward):
            if not finish:
                link(n, target, n, n).wait_recv()

            @pl.when(forward)
            def _():
                copy = link(n, target, n, jnp.minimum(n + 2, end))
                copy.wait_send() if finish else copy.start()

            copy = cross(n)
            copy.wait_send() if finish else copy.start()

        @pl.when(s < last)
        def _():
            arrive(2 * s - 1, up, jnp.logical_or(s < last - 1, parity == 0))
            arrive(2 * s, down, jnp.logical_or(s < last - 1, parity == 1))

        @pl.when(s == last)
        def _():
            if not finish:
                link(end, up, end, end).wait_recv()
            copy = cross(end)
            copy.wait_send() if finish else copy.start()

    def chunk_comm(q, s, finish):
        comm(
            q, s, lax.rem(q, 2),
            lambda n, target, index, arrival: ring(q, n, target, index, arrival),
            lambda n: across(q, n), finish,
        )

    def x_comm(s, finish):
        comm(s * 0, s, s * 0, x_ring, x_across, finish)

    def pick(q):
        chosen = pick_ref[pl.ds(q, 1), :]

        def part(k, carry):
            start = pl.multiple_of(k * panel, panel)
            spots = lax.broadcasted_iota(jnp.int32, (panel, chunk), 0) + start
            hot = jnp.where(spots == chosen, 1.0, 0.0).astype(BF16)
            piece = dot(d[:, pl.ds(start, panel)], hot, (1, 0))

            @pl.when(k == 0)
            def _():
                kacc[...] = piece

            @pl.when(k > 0)
            def _():
                kacc[...] += piece

            return carry

        lax.fori_loop(0, PARTS, part, 0)
        a[me, pl.ds(pl.multiple_of(q * chunk, chunk), chunk), :] = kacc[...].T.astype(BF16)

    def permute(i):
        n = lax.div(i, 2)
        b = 2 * place(n) + lax.rem(i, 2)
        wanted = jnp.broadcast_to(perm_ref[pl.ds(b, 1), :], (128, rows)).T[:, :1]

        def part(k, carry):
            start = pl.multiple_of(k * order, order)
            spots = lax.broadcasted_iota(jnp.int32, (rows, order), 1) + start
            hot = jnp.where(spots == wanted, 1.0, 0.0).astype(BF16)
            piece = dot(hot, e[pl.ds(start, order), :], (1, 0))

            @pl.when(k == 0)
            def _():
                pacc[...] = piece

            @pl.when(k > 0)
            def _():
                pacc[...] += piece

            return carry

        lax.fori_loop(0, PARTS, part, 0)
        m[i] = pacc[...].astype(BF16)
        some = e[pl.ds(pl.multiple_of(i * rows, rows), rows), :].astype(F32)
        pn_ref[...] += jnp.sum(some * some, axis=0, keepdims=True)

    def add(q, slot, n):
        across(q, n).wait_recv()
        at = 2 * place(n)
        start = pl.ds(pl.multiple_of(q * chunk, chunk), chunk)
        one, two = a[at, start, :], a[at + 1, start, :]
        acc[slot] += dot(one, m[2 * n], (1, 0)) + dot(two, m[2 * n + 1], (1, 0))
        lac[slot] += dot(one, xt[at], (1, 1)) + dot(two, xt[at + 1], (1, 1))
        one, two = one.astype(F32), two.astype(F32)
        total = one * one + two * two
        sq[slot] += sum(total[:, c : c + 128] for c in range(0, rows, 128)) if rows > 128 else total

    def clear(slot):
        acc[slot] = jnp.zeros(acc.shape[1:], F32)
        lac[slot] = jnp.zeros(lac.shape[1:], F32)
        sq[slot] = jnp.zeros(sq.shape[1:], F32)

    def emit(q, slot):
        return pltpu.make_async_copy(
            acc.at[slot], out_hbm.at[pl.ds(pl.multiple_of(q * chunk, chunk), chunk), :], out_sem.at[q]
        )

    def finish_chunk(q, slot):
        loads = lac[slot]
        white = dot(loads, gram[...], (1, 0), HIGHEST)
        norm = jnp.sum(sq[slot], axis=1, keepdims=True) + jnp.sum(white * loads, axis=1, keepdims=True)
        norm = jnp.maximum(norm, 0.0)
        fitted = dot(loads, h[...], (1, 0), HIGHEST)
        acc[slot] = (acc[slot] + fitted) * (scale * lax.rsqrt(norm + epsilon))
        emit(q, slot).start()

    def sweep(k, carry):
        whole = gram[...]
        row = gram[pl.ds(k, 1), :]
        here = lax.broadcasted_iota(jnp.int32, whole.shape, 1) == k
        there = lax.broadcasted_iota(jnp.int32, whole.shape, 0) == k
        column = jnp.sum(jnp.where(here, whole, 0.0), axis=1, keepdims=True)
        corner = jnp.sum(jnp.where(here[:1], row, 0.0), axis=1, keepdims=True)
        inverse = 1.0 / corner
        scaled = row * inverse
        inner = jnp.where(here, column * inverse, whole - column * scaled)
        gram[...] = jnp.where(there, jnp.where(here, -inverse, scaled), inner)
        return carry

    def loop(first, final, body):
        def step(k, carry):
            body(k)
            return carry

        lax.fori_loop(first, final, step, 0)

    load_d = pltpu.make_async_copy(d_hbm, d, load_sem.at[0])
    load_e = pltpu.make_async_copy(e_hbm, e, load_sem.at[1])
    load_d.start()
    load_e.start()
    barrier = pltpu.get_barrier_semaphore()
    for other in (up, down, sib):
        pl.semaphore_signal(barrier, inc=1, device_id={"samp": other}, device_id_type=MESH)
    xt[me] = xt_ref[...]
    pn_ref[...] = jnp.zeros(pn_ref.shape, F32)
    pl.semaphore_wait(barrier, 3)
    zero = me * 0
    for copy in (x_ring(zero, up, 0, 1), x_ring(zero, down, half, 2), x_across(zero)):
        copy.start()
    load_d.wait()

    def first_picks(q):
        pick(q)
        for copy in own(q):
            copy.start()

    loop(0, 2, first_picks)
    load_e.wait()

    ticks = 2 * last
    total = 4 * ticks

    def tick(t):
        p = lax.div(t, ticks)
        s = lax.div(lax.rem(t, ticks), 2) + 1
        j = lax.rem(t, 2)
        q = 2 * p + j
        chunk_comm(q, s, False)

        @pl.when(jnp.logical_and(t < ticks, j == 0))
        def _():
            x_comm(s, False)

        five, left = lax.div(t, 5), lax.rem(t, 5)

        @pl.when(jnp.logical_and(t < 40, left < 4))
        def _():
            permute(4 * five + left)

        @pl.when(jnp.logical_and(jnp.logical_and(t < 40, left == 4), lax.rem(five, 3) < 2))
        def _():
            first_picks(2 + five - lax.div(five, 3))

        @pl.when(t >= ticks)
        def _():
            chunk_comm(q - 2, s, True)

        @pl.when(t == 29)
        def _():
            gram[...] = jnp.zeros(gram.shape, F32)

            def side(n):
                x_across(n).wait_recv()
                at = 2 * place(n)
                one, two = xt[at], xt[at + 1]
                gram[...] += dot(one, one, (1, 1)) + dot(two, two, (1, 1))

            loop(0, half, side)
            xtm[...] = jnp.zeros(xtm.shape, F32)

        @pl.when(jnp.logical_and(t >= 40, t < 48))
        def _():
            each = covars // 8
            lax.fori_loop((t - 40) * each, (t - 39) * each, sweep, 0)

            def side(n):
                at = 2 * place(n)
                xtm[...] += dot(xt[at], m[2 * n], (1, 0)) + dot(xt[at + 1], m[2 * n + 1], (1, 0))

            loop(2 * (t - 40), 2 * (t - 39), side)

        @pl.when(t == 48)
        def _():
            h[...] = dot(gram[...], xtm[...], (1, 0), HIGHEST)

        @pl.when(t >= 40)
        def _():
            q_old = lax.div(t - 40, 4)
            quarter = lax.rem(t - 40, 4)
            slot = lax.rem(q_old, 3)

            @pl.when(quarter == 0)
            def _():
                @pl.when(q_old >= 3)
                def _():
                    emit(q_old - 3, slot).wait()

                clear(slot)

            loop(4 * quarter, 4 * quarter + 4, lambda n: add(q_old, slot, n))

        @pl.when(t >= 48)
        def _():
            @pl.when(s == 1)
            def _():
                clear(3 + j)

            loop(jnp.maximum(2 * s - 3, 0), 2 * s - 1, lambda n: add(6 + j, 3 + j, n))

        early = jnp.logical_or(t == 49, t == 50)
        regular = jnp.logical_and(t >= 51, lax.rem(t, 4) == 3)

        @pl.when(jnp.logical_or(early, regular))
        def _():
            q_done = jnp.where(early, t - 49, lax.div(t - 43, 4))
            finish_chunk(q_done, lax.rem(q_done, 3))

    loop(0, total, tick)

    def tail(j):
        add(6 + j, 3 + j, end)
        finish_chunk(6 + j, 3 + j)

    loop(0, 2, tail)

    def retire(t):
        s = lax.div(t, 2) + 1
        chunk_comm(6 + lax.rem(t, 2), s, True)

    loop(0, ticks, retire)
    loop(1, last + 1, lambda s: x_comm(s, True))
    for copy in (x_ring(zero, up, 0, 1), x_ring(zero, down, half, 2), x_across(zero)):
        copy.wait_send()

    def retire_own(q):
        for copy in own(q):
            copy.wait_send()

    loop(0, CHUNKS, retire_own)
    loop(3, 8, lambda q: emit(q, jnp.where(q < 6, q - 3, q - 3)).wait())


def local(length, dosage, covariates, expression, block_index, expr_row):
    blocks, width = block_index.shape
    rows, panel = dosage.shape
    covars = covariates.shape[1]
    samples, genes = expression.shape
    wide = blocks * width
    chunk = wide // CHUNKS
    half = length // 2
    scale = math.sqrt(samples - covars - 1)
    vmem = pl.BlockSpec(memory_space=pltpu.VMEM)
    dma = pltpu.SemaphoreType.DMA
    products, panel_norm = pl.pallas_call(
        lambda *refs: scan_kernel(scale, length, *refs),
        out_shape=(
            jax.ShapeDtypeStruct((wide, genes), F32),
            jax.ShapeDtypeStruct((1, genes), F32),
        ),
        in_specs=[pl.BlockSpec(memory_space=pl.ANY)] * 2 + [vmem] * 3,
        out_specs=(pl.BlockSpec(memory_space=pl.ANY), vmem),
        scratch_shapes=[
            pltpu.VMEM((length, wide, rows), BF16),
            pltpu.VMEM((length, covars, rows), BF16),
            pltpu.VMEM((samples, genes), BF16),
            pltpu.VMEM((length, rows, genes), BF16),
            pltpu.VMEM((rows, panel), BF16),
            pltpu.VMEM((5, chunk, genes), F32),
            pltpu.VMEM((5, chunk, covars), F32),
            pltpu.VMEM((5, chunk, min(rows, 128)), F32),
            pltpu.VMEM((rows, genes), F32),
            pltpu.VMEM((rows, chunk), F32),
            pltpu.VMEM((covars, covars), F32),
            pltpu.VMEM((covars, genes), F32),
            pltpu.VMEM((covars, genes), F32),
            dma((CHUNKS, half + 1)),
            dma((CHUNKS, half)),
            dma((CHUNKS, half)),
            dma((CHUNKS, half)),
            dma((half + 1,)),
            dma((half,)),
            dma((half,)),
            dma((half,)),
            dma((2,)),
            dma((CHUNKS,)),
        ],
        compiler_params=pltpu.CompilerParams(
            collective_id=0, has_side_effects=True, vmem_limit_bytes=67000000
        ),
        name="scan",
    )(
        dosage, expression, covariates.T,
        block_index.reshape(CHUNKS, chunk), expr_row.reshape(length, rows),
    )
    return products * lax.rsqrt(panel_norm + epsilon)


def solution(mesh):
    length = mesh.shape["samp"]
    both = ("groups", "samp")
    in_specs = (P(both, None), P(both, None), P("groups", "samp"), P("groups", None), P("groups"))
    return jax.shard_map(
        lambda *args: local(length, *args), mesh=mesh, in_specs=in_specs, out_specs=P("groups", "samp"), check_vma=False
    )
```

profile of v0, /device:TPU:69, one launch (start us, length us, event | category | flops | bytes accessed | tf_op | source)
XLA Modules:
  0.0 251.3 jit_solution(2889033965401543915)
XLA Ops:
  0.0 1.3 reshape.6.refs_3_
  1.3 1.4 reshape.7.refs_4_
  2.7 243.3 %scan.1 = (f32[2048,512]{1,0:T(8,128)}, f32[1,512]{1,0:T(1,128)}) custom-call(bf16[256,8192]{1,0:T(8,128)(2,1)} %refs_0_.1, bf16[8192,512]{1,0:T(8,128)(2,1)} %refs_1_.1, bf16[96,256]{1,0:T(8,128)(2,1)} %bitcast.2, s32[8,256]{1,0:T(8,128)} %reshape.6.refs_3_, s32[32,256]{1,0:T(8,128)} %reshape.7.refs_4_), custom_call_target="tpu_custom_call" | custom-call | tf_op jit(solution)/shard_map/scan/pallas_call | solution.py:366
  245.9 0.7 add_rsqrt_fusion
  246.6 4.7 %broadcast_multiply_fusion = f32[2048,512]{1,0:T(8,128)} fusion(f32[2048,512]{1,0:T(8,128)} %get-tuple-element.7, f32[512]{0:T(512)S(1)} %bitcast.3), kind=kLoop, calls=%fused_computation | loop fusion | flops 1048576 | bytes 8390656 | tf_op jit(solution)/shard_map/mul | solution.py:407
where the time goes:
time: 254 us; the launch traced here: 251 us
  Pallas kernels  243 us (96%)
  other arithmetic  5.4 us (2%)
  local copies, waits for them, and re-layouts  2.68 us (1%)
    pallas_call x1, Pallas kernels, local(): pl.pallas_call(lambda *refs: scan_kernel(scale, length, *refs), out_shape...  243 us

commit v1 on v0

v1 whole, which is shorter than its diff:
```python
import math

import jax
import jax.numpy as jnp
from jax import lax
from jax.experimental import pallas as pl
from jax.experimental.pallas import tpu as pltpu
from jax.sharding import PartitionSpec as P

MESH = pl.DeviceIdType.MESH
HIGHEST = lax.Precision.HIGHEST
F32 = jnp.float32
BF16 = jnp.bfloat16
epsilon = 1e-06
CHUNKS = 4
PARTS = 4


def dot(a, b, contract, precision=None):
    return lax.dot_general(
        a, b, ((contract[:1], contract[1:]), ((), ())), precision=precision, preferred_element_type=F32
    )


def scan_kernel(
    scale, length, per,
    d_hbm, e_hbm, xt_ref, pick_ref, perm_ref,
    out_hbm, pn_ref,
    a, xt, e, m, d, acc, lac, sq, wanted, kacc, gram, xtm, h,
    ring_send, ring_recv, sib_send, sib_recv, x_send, x_recv, xs_send, xs_recv, load_sem, out_sem,
):
    half = length // 2
    last = half // 2
    end = half - 1
    me = lax.axis_index("samp")
    z = lax.div(me, 2)
    core = lax.rem(me, 2)
    up = lax.rem(me + 2, length)
    down = lax.rem(me + length - 2, length)
    sib = me + 1 - 2 * core
    zero = me * 0
    chunk = a.shape[1] // CHUNKS
    rows = a.shape[2]
    pair = 2 * rows
    covars = xt.shape[1]
    panel = d.shape[1] // PARTS
    ring_slots = m.shape[0]

    def place(n):
        s = lax.div(n + 1, 2)
        sign = 2 * lax.rem(n + 1, 2) - 1
        return lax.rem(z + sign * s + half, half)

    def span(q):
        return pl.ds(pl.multiple_of(q * chunk, chunk), chunk)

    def ring(q, n, target, index, arrival):
        ref = a.at[2 * place(n) + core, span(q), :]
        return pltpu.make_async_remote_copy(
            src_ref=ref, dst_ref=ref, send_sem=ring_send.at[q, index], recv_sem=ring_recv.at[q, arrival],
            device_id={"samp": target}, device_id_type=MESH,
        )

    def across(q, n):
        ref = a.at[2 * place(n) + core, span(q), :]
        return pltpu.make_async_remote_copy(
            src_ref=ref, dst_ref=ref, send_sem=sib_send.at[q, n], recv_sem=sib_recv.at[q, n],
            device_id={"samp": sib}, device_id_type=MESH,
        )

    def x_ring(n, target, index, arrival):
        ref = xt.at[2 * place(n) + core]
        return pltpu.make_async_remote_copy(
            src_ref=ref, dst_ref=ref, send_sem=x_send.at[index], recv_sem=x_recv.at[arrival],
            device_id={"samp": target}, device_id_type=MESH,
        )

    def x_across(n):
        ref = xt.at[2 * place(n) + core]
        return pltpu.make_async_remote_copy(
            src_ref=ref, dst_ref=ref, send_sem=xs_send.at[n], recv_sem=xs_recv.at[n],
            device_id={"samp": sib}, device_id_type=MESH,
        )

    def own(q):
        return (ring(q, 0, up, 0, 1), ring(q, 0, down, half, 2), across(q, 0))

    def own_x():
        return (x_ring(zero, up, 0, 1), x_ring(zero, down, half, 2), x_across(zero))

    def comm(s, parity, link, cross, finish):
        def arrive(n, target, forward):
            if not finish:
                link(n, target, n, n).wait_recv()

            @pl.when(forward)
            def _():
                copy = link(n, target, n, jnp.minimum(n + 2, end))
                copy.wait_send() if finish else copy.start()

            copy = cross(n)
            copy.wait_send() if finish else copy.start()

        @pl.when(s < last)
        def _():
            arrive(2 * s - 1, up, jnp.logical_or(s < last - 1, parity == 0))
            arrive(2 * s, down, jnp.logical_or(s < last - 1, parity == 1))

        @pl.when(s == last)
        def _():
            if not finish:
                link(end, up, end, end).wait_recv()
            copy = cross(end)
            copy.wait_send() if finish else copy.start()

    def chunk_comm(q, s, finish=False):
        comm(
            s, lax.rem(q, 2),
            lambda n, target, index, arrival: ring(q, n, target, index, arrival),
            lambda n: across(q, n), finish,
        )

    def x_comm(s, finish=False):
        comm(s, zero, x_ring, x_across, finish)

    def loop(first, final, body):
        def step(k, carry):
            body(k)
            return carry

        lax.fori_loop(first, final, step, 0)

    def load_d(k):
        part = pl.ds(pl.multiple_of(k * panel, panel), panel)
        return pltpu.make_async_copy(d_hbm.at[:, part], d.at[:, part], load_sem.at[k])

    load_e = pltpu.make_async_copy(e_hbm, e, load_sem.at[PARTS])

    def pick(q):
        chosen = pick_ref[pl.ds(lax.div(q, per), 1), span(lax.rem(q, per))]

        def part(k):
            @pl.when(q == 0)
            def _():
                load_d(k).wait()

            start = pl.multiple_of(k * panel, panel)
            spots = lax.broadcasted_iota(jnp.int32, (panel, chunk), 0)
            hot = jnp.where(spots == chosen - start, 1.0, 0.0).astype(BF16)
            piece = dot(d[:, pl.ds(start, panel)], hot, (1, 0))

            @pl.when(k == 0)
            def _():
                kacc[...] = piece

            @pl.when(k > 0)
            def _():
                kacc[...] += piece

        loop(0, PARTS, part)
        a[me, span(q), :] = kacc[...].T.astype(BF16)
        for copy in own(q):
            copy.start()

    def permute(n):
        here = pl.ds(pl.multiple_of(place(n) * pair, pair), pair)
        wanted[...] = jnp.broadcast_to(perm_ref[:, here], (128, pair)).T

        def part(c):
            mine = pl.ds(pl.multiple_of(c * rows, rows), rows)
            spots = lax.broadcasted_iota(jnp.int32, (rows, e.shape[0]), 1)
            hot = jnp.where(spots == wanted[mine, :1], 1.0, 0.0).astype(BF16)
            m[lax.rem(n, ring_slots), mine, :] = dot(hot, e[...], (1, 0)).astype(BF16)

        loop(0, 2, part)
        some = e[pl.ds(pl.multiple_of(n * pair, pair), pair), :].astype(F32)
        pn_ref[...] += jnp.sum(some * some, axis=0, keepdims=True)

    def matched(n):
        both = m[lax.rem(n, ring_slots)]
        return both[:rows], both[rows:]

    def add(q, spots):
        blocks = []
        for n in spots:
            across(q, n).wait_recv()
            at = 2 * place(n)
            mine = matched(n)
            blocks += [(a[at + c, span(q), :], mine[c], xt[at + c]) for c in range(2)]
        acc[q] += sum(dot(block, rest, (1, 0)) for block, rest, _ in blocks)
        lac[q] += sum(dot(block, side, (1, 1)) for block, _, side in blocks)
        total = sum(jnp.square(block.astype(F32)) for block, _, _ in blocks)
        sq[q] += sum(total[:, c : c + sq.shape[2]] for c in range(0, rows, sq.shape[2]))

    def side(n):
        at = 2 * place(n)
        one, two = matched(n)
        xtm[...] += dot(xt[at], one, (1, 0)) + dot(xt[at + 1], two, (1, 0))

    def emit(q):
        return pltpu.make_async_copy(acc.at[q], out_hbm.at[span(q), :], out_sem.at[q])

    def finish_chunk(q):
        loads = lac[q]
        white = dot(loads, gram[...], (1, 0), HIGHEST)
        norm = jnp.sum(sq[q], axis=1, keepdims=True) + jnp.sum(white * loads, axis=1, keepdims=True)
        norm = jnp.maximum(norm, 0.0)
        fitted = dot(loads, h[...], (1, 0), HIGHEST)
        acc[q] = (acc[q] + fitted) * (scale * lax.rsqrt(norm + epsilon))
        emit(q).start()

    def sweep(k):
        whole = gram[...]
        row = gram[pl.ds(k, 1), :]
        here = lax.broadcasted_iota(jnp.int32, whole.shape, 1) == k
        there = lax.broadcasted_iota(jnp.int32, whole.shape, 0) == k
        column = jnp.sum(jnp.where(here, whole, 0.0), axis=1, keepdims=True)
        corner = jnp.sum(jnp.where(here[:1], row, 0.0), axis=1, keepdims=True)
        inverse = 1.0 / corner
        scaled = row * inverse
        inner = jnp.where(here, column * inverse, whole - column * scaled)
        gram[...] = jnp.where(there, jnp.where(here, -inverse, scaled), inner)

    loop(0, PARTS, lambda k: load_d(k).start())
    load_e.start()
    barrier = pltpu.get_barrier_semaphore()
    for other in (up, down, sib):
        pl.semaphore_signal(barrier, inc=1, device_id={"samp": other}, device_id_type=MESH)
    xt[me] = xt_ref[...]
    pl.semaphore_wait(barrier, 3)
    for copy in own_x():
        copy.start()
    loop(0, CHUNKS, pick)
    for ref in (acc, lac, sq, gram, xtm, pn_ref):
        ref[...] = jnp.zeros(ref.shape, F32)
    load_e.wait()
    loop(0, 2, permute)

    ticks = CHUNKS * (last - 1)
    per_tick = covars // 16

    def tick(t):
        s = lax.div(t, CHUNKS) + 1
        j = lax.rem(t, CHUNKS)
        chunk_comm(j, s)

        @pl.when(t < last)
        def _():
            x_comm(t + 1)

        @pl.when(lax.rem(j, 2) == 0)
        def _():
            permute(2 * s + lax.div(j, 2))

        @pl.when(jnp.logical_and(j == 1, s == 1))
        def _():
            x_across(zero).wait_recv()
            side(zero)

        @pl.when(jnp.logical_and(j == 1, s > 1))
        def _():
            @pl.when(s == 2)
            def _():
                loop(1, 3, lambda n: x_across(n).wait_recv())

            loop(2 * s - 3, 2 * s - 1, side)

        @pl.when(jnp.logical_and(lax.rem(j, 2) == 1, s == 1))
        def _():
            loop(j - 1, j + 1, lambda q: add(q, (zero,)))

        @pl.when(jnp.logical_and(lax.rem(j, 2) == 1, s > 1))
        def _():
            loop(j - 1, j + 1, lambda q: add(q, (2 * s - 3, 2 * s - 2)))

        @pl.when(s >= 3)
        def _():
            chunk_comm(j, s - 2, True)

        @pl.when(s == 3)
        def _():
            for copy in own(j):
                copy.wait_send()

        @pl.when(jnp.logical_and(t >= last, t < 2 * last))
        def _():
            x_comm(t - last + 1, True)

        @pl.when(t == last)
        def _():
            for copy in own_x():
                copy.wait_send()

            loop(3, half, lambda n: x_across(n).wait_recv())

            def square(n):
                at = 2 * place(n)
                one, two = xt[at], xt[at + 1]
                gram[...] += dot(one, one, (1, 1)) + dot(two, two, (1, 1))

            loop(0, half, square)

        @pl.when(jnp.logical_and(t > last, t <= last + 16))
        def _():
            loop((t - last - 1) * per_tick, (t - last) * per_tick, sweep)

    loop(0, ticks, tick)

    loop(end - 2, end + 1, side)
    h[...] = dot(gram[...], xtm[...], (1, 0), HIGHEST)
    loop(0, CHUNKS, lambda q: add(q, (zero + end - 2, zero + end - 1)))

    def closing(k):
        first, final = 2 * k, 2 * k + 2
        loop(first, final, lambda q: chunk_comm(q, zero + last))

        def close(q):
            add(q, (zero + end,))
            finish_chunk(q)

        loop(first, final, close)
        loop(0, CHUNKS, lambda q: chunk_comm(q, last - 2 + k, True))

    loop(0, CHUNKS // 2, closing)
    loop(0, CHUNKS, lambda q: chunk_comm(q, zero + last, True))
    loop(0, CHUNKS, lambda q: emit(q).wait())


def local(length, dosage, covariates, expression, block_index, expr_row):
    blocks, width = block_index.shape
    rows, panel = dosage.shape
    covars = covariates.shape[1]
    samples, genes = expression.shape
    wide = blocks * width
    chunk = wide // CHUNKS
    half = length // 2
    scale = math.sqrt(samples - covars - 1)
    vmem = pl.BlockSpec(memory_space=pltpu.VMEM)
    dma = pltpu.SemaphoreType.DMA
    products, panel_norm = pl.pallas_call(
        lambda *refs: scan_kernel(scale, length, CHUNKS // blocks, *refs),
        out_shape=(
            jax.ShapeDtypeStruct((wide, genes), F32),
            jax.ShapeDtypeStruct((1, genes), F32),
        ),
        in_specs=[pl.BlockSpec(memory_space=pl.ANY)] * 2 + [vmem] * 3,
        out_specs=(pl.BlockSpec(memory_space=pl.ANY), vmem),
        scratch_shapes=[
            pltpu.VMEM((length, wide, rows), BF16),
            pltpu.VMEM((length, covars, rows), BF16),
            pltpu.VMEM((samples, genes), BF16),
            pltpu.VMEM((8, 2 * rows, genes), BF16),
            pltpu.VMEM((rows, panel), BF16),
            pltpu.VMEM((CHUNKS, chunk, genes), F32),
            pltpu.VMEM((CHUNKS, chunk, covars), F32),
            pltpu.VMEM((CHUNKS, chunk, min(rows, 128)), F32),
            pltpu.VMEM((2 * rows, 128), jnp.int32),
            pltpu.VMEM((rows, chunk), F32),
            pltpu.VMEM((covars, covars), F32),
            pltpu.VMEM((covars, genes), F32),
            pltpu.VMEM((covars, genes), F32),
            dma((CHUNKS, half + 1)),
            dma((CHUNKS, half)),
            dma((CHUNKS, half)),
            dma((CHUNKS, half)),
            dma((half + 1,)),
            dma((half,)),
            dma((half,)),
            dma((half,)),
            dma((PARTS + 1,)),
            dma((CHUNKS,)),
        ],
        compiler_params=pltpu.CompilerParams(
            collective_id=0, has_side_effects=True, vmem_limit_bytes=67000000
        ),
        name="scan",
    )(
        dosage, expression, covariates.T,
        block_index, expr_row.reshape(1, samples),
    )
    return products * lax.rsqrt(panel_norm + epsilon)


def solution(mesh):
    length = mesh.shape["samp"]
    both = ("groups", "samp")
    in_specs = (P(both, None), P(both, None), P("groups", "samp"), P("groups", None), P("groups"))
    return jax.shard_map(
        lambda *args: local(length, *args), mesh=mesh, in_specs=in_specs, out_specs=P("groups", "samp"), check_vma=False
    )
```

time: 254 us -> 216 us (0.85)
  Pallas kernels: 243 us -> 210 us
  local copies, waits for them, and re-layouts: 2.68 us -> 0 us
    pallas_call x1, Pallas kernels: 243 us -> 210 us  [local(): pl.pallas_call(lambda *refs: scan_kernel(scale, length, CHUNKS // blocks,...]
    reshape x2 -> x0, local copies, waits for them, and re-layouts: 2.68 us -> none  [the longest x1 1.38 us: local(): expr_row.reshape(length, rows)]
where the time goes in v1:
time: 216 us
  Pallas kernels  210 us (97%)
  other arithmetic  5.39 us (2%)
    pallas_call x1, Pallas kernels, local(): pl.pallas_call(lambda *refs: scan_kernel(scale, length, CHUNKS // blocks,...  210 us
    mul x1, other arithmetic, local(): return products * lax.rsqrt(panel_norm + epsilon)  4.72 us

profile of v1, /device:TPU:69, one launch (start us, length us, event | category | flops | bytes accessed | tf_op | source)
XLA Modules:
  0.0 215.7 jit_solution(11827357106213446599)
XLA Ops:
  0.0 210.3 %scan.1 = (f32[2048,512]{1,0:T(8,128)}, f32[1,512]{1,0:T(1,128)}) custom-call(bf16[256,8192]{1,0:T(8,128)(2,1)} %refs_0_.1, bf16[8192,512]{1,0:T(8,128)(2,1)} %refs_1_.1, bf16[96,256]{1,0:T(8,128)(2,1)} %bitcast.3, s32[2,1024]{1,0:T(2,128)} %refs_3_.1, s32[1,8192]{1,0:T(1,128)} %bitcast.4), custom_call_target="tpu_custom_call" | custom-call | tf_op jit(solution)/shard_map/scan/pallas_call | solution.py:340
  210.3 0.7 add_rsqrt_fusion
  211.0 4.7 %broadcast_multiply_fusion = f32[2048,512]{1,0:T(8,128)} fusion(f32[2048,512]{1,0:T(8,128)} %get-tuple-element.7, f32[512]{0:T(512)S(1)} %bitcast.5), kind=kLoop, calls=%fused_computation | loop fusion | flops 1048576 | bytes 8390656 | tf_op jit(solution)/shard_map/mul | solution.py:381

commit v2 on v1

--- a/solution.py
+++ b/solution.py
@@ -25,9 +25,9 @@
 def scan_kernel(
     scale, length, per,
     d_hbm, e_hbm, xt_ref, pick_ref, perm_ref,
-    out_hbm, pn_ref,
-    a, xt, e, m, d, acc, lac, sq, wanted, kacc, gram, xtm, h,
-    ring_send, ring_recv, sib_send, sib_recv, x_send, x_recv, xs_send, xs_recv, load_sem, out_sem,
+    out_ref,
+    a, xt, e, m, d, lac, sq, wanted, kacc, gram, xtm, both, pn_ref,
+    ring_send, ring_recv, sib_send, sib_recv, x_send, x_recv, xs_send, xs_recv, load_sem,
 ):
     half = length // 2
     last = half // 2
@@ -187,7 +187,7 @@
             at = 2 * place(n)
             mine = matched(n)
             blocks += [(a[at + c, span(q), :], mine[c], xt[at + c]) for c in range(2)]
-        acc[q] += sum(dot(block, rest, (1, 0)) for block, rest, _ in blocks)
+        out_ref[span(q), :] += sum(dot(block, rest, (1, 0)) for block, rest, _ in blocks)
         lac[q] += sum(dot(block, side, (1, 1)) for block, _, side in blocks)
         total = sum(jnp.square(block.astype(F32)) for block, _, _ in blocks)
         sq[q] += sum(total[:, c : c + sq.shape[2]] for c in range(0, rows, sq.shape[2]))
@@ -197,17 +197,15 @@
         one, two = matched(n)
         xtm[...] += dot(xt[at], one, (1, 0)) + dot(xt[at + 1], two, (1, 0))
 
-    def emit(q):
-        return pltpu.make_async_copy(acc.at[q], out_hbm.at[span(q), :], out_sem.at[q])
-
     def finish_chunk(q):
         loads = lac[q]
-        white = dot(loads, gram[...], (1, 0), HIGHEST)
+        change = dot(loads, both[...], (1, 0), HIGHEST)
+        genes = xtm.shape[1]
+        fitted, white = change[:, :genes], change[:, genes : genes + covars]
         norm = jnp.sum(sq[q], axis=1, keepdims=True) + jnp.sum(white * loads, axis=1, keepdims=True)
         norm = jnp.maximum(norm, 0.0)
-        fitted = dot(loads, h[...], (1, 0), HIGHEST)
-        acc[q] = (acc[q] + fitted) * (scale * lax.rsqrt(norm + epsilon))
-        emit(q).start()
+        row, column = scale * lax.rsqrt(norm + epsilon), lax.rsqrt(pn_ref[...] + epsilon)
+        out_ref[span(q), :] = (out_ref[span(q), :] + fitted) * row * column
 
     def sweep(k):
         whole = gram[...]
@@ -221,17 +219,18 @@
         inner = jnp.where(here, column * inverse, whole - column * scaled)
         gram[...] = jnp.where(there, jnp.where(here, -inverse, scaled), inner)
 
-    loop(0, PARTS, lambda k: load_d(k).start())
-    load_e.start()
     barrier = pltpu.get_barrier_semaphore()
     for other in (up, down, sib):
         pl.semaphore_signal(barrier, inc=1, device_id={"samp": other}, device_id_type=MESH)
+    loop(0, PARTS, lambda k: load_d(k).start())
     xt[me] = xt_ref[...]
     pl.semaphore_wait(barrier, 3)
     for copy in own_x():
         copy.start()
-    loop(0, CHUNKS, pick)
-    for ref in (acc, lac, sq, gram, xtm, pn_ref):
+    pick(zero)
+    load_e.start()
+    loop(1, CHUNKS, pick)
+    for ref in (out_ref, lac, sq, gram, xtm, both, pn_ref):
         ref[...] = jnp.zeros(ref.shape, F32)
     load_e.wait()
     loop(0, 2, permute)
@@ -307,7 +306,8 @@
     loop(0, ticks, tick)
 
     loop(end - 2, end + 1, side)
-    h[...] = dot(gram[...], xtm[...], (1, 0), HIGHEST)
+    both[:, : xtm.shape[1]] = dot(gram[...], xtm[...], (1, 0), HIGHEST)
+    both[:, xtm.shape[1] : xtm.shape[1] + covars] = gram[...]
     loop(0, CHUNKS, lambda q: add(q, (zero + end - 2, zero + end - 1)))
 
     def closing(k):
@@ -323,7 +323,6 @@
 
     loop(0, CHUNKS // 2, closing)
     loop(0, CHUNKS, lambda q: chunk_comm(q, zero + last, True))
-    loop(0, CHUNKS, lambda q: emit(q).wait())
 
 
 def local(length, dosage, covariates, expression, block_index, expr_row):
@@ -337,28 +336,25 @@
     scale = math.sqrt(samples - covars - 1)
     vmem = pl.BlockSpec(memory_space=pltpu.VMEM)
     dma = pltpu.SemaphoreType.DMA
-    products, panel_norm = pl.pallas_call(
+    return pl.pallas_call(
         lambda *refs: scan_kernel(scale, length, CHUNKS // blocks, *refs),
-        out_shape=(
-            jax.ShapeDtypeStruct((wide, genes), F32),
-            jax.ShapeDtypeStruct((1, genes), F32),
-        ),
+        out_shape=pltpu.VMEM((wide, genes), F32),
         in_specs=[pl.BlockSpec(memory_space=pl.ANY)] * 2 + [vmem] * 3,
-        out_specs=(pl.BlockSpec(memory_space=pl.ANY), vmem),
+        out_specs=vmem,
         scratch_shapes=[
             pltpu.VMEM((length, wide, rows), BF16),
             pltpu.VMEM((length, covars, rows), BF16),
             pltpu.VMEM((samples, genes), BF16),
             pltpu.VMEM((8, 2 * rows, genes), BF16),
             pltpu.VMEM((rows, panel), BF16),
-            pltpu.VMEM((CHUNKS, chunk, genes), F32),
             pltpu.VMEM((CHUNKS, chunk, covars), F32),
             pltpu.VMEM((CHUNKS, chunk, min(rows, 128)), F32),
             pltpu.VMEM((2 * rows, 128), jnp.int32),
             pltpu.VMEM((rows, chunk), F32),
             pltpu.VMEM((covars, covars), F32),
             pltpu.VMEM((covars, genes), F32),
-            pltpu.VMEM((covars, genes), F32),
+            pltpu.VMEM((covars, genes + 128), F32),
+            pltpu.VMEM((1, genes), F32),
             dma((CHUNKS, half + 1)),
             dma((CHUNKS, half)),
             dma((CHUNKS, half)),
@@ -368,17 +364,15 @@
             dma((half,)),
             dma((half,)),
             dma((PARTS + 1,)),
-            dma((CHUNKS,)),
         ],
         compiler_params=pltpu.CompilerParams(
-            collective_id=0, has_side_effects=True, vmem_limit_bytes=67000000
+            collective_id=0, has_side_effects=True, vmem_limit_bytes=62000000
         ),
         name="scan",
     )(
         dosage, expression, covariates.T,
         block_index, expr_row.reshape(1, samples),
     )
-    return products * lax.rsqrt(panel_norm + epsilon)
 
 
 def solution(mesh):

time: 216 us -> 212 us (0.981)
  other arithmetic: 5.39 us -> 0 us
    mul x1 -> x0, other arithmetic: 4.72 us -> none  [local(): return products * lax.rsqrt(panel_norm + epsilon)]
where the time goes in v2:
time: 212 us
  Pallas kernels  210 us (99%)
    pallas_call x1, Pallas kernels, local(): pl.pallas_call(lambda *refs: scan_kernel(scale, length, CHUNKS // blocks,...  210 us

profile of v2, /device:TPU:69, one launch (start us, length us, event | category | flops | bytes accessed | tf_op | source)
XLA Modules:
  0.0 211.6 jit_solution(3250256505286721241)
XLA Ops:
  0.0 209.5 %scan.1 = f32[2048,512]{1,0:T(8,128)S(1)} custom-call(bf16[256,8192]{1,0:T(8,128)(2,1)} %refs_0_.1, bf16[8192,512]{1,0:T(8,128)(2,1)} %refs_1_.1, bf16[96,256]{1,0:T(8,128)(2,1)} %bitcast.2, s32[2,1024]{1,0:T(2,128)} %refs_3_.1, s32[1,8192]{1,0:T(1,128)} %bitcast.3), custom_call_target="tpu_custom_call" | custom-call | tf_op jit(solution)/shard_map/scan/pallas_call | solution.py:339
  209.5 2.0 copy.7

commit v3 on v2

--- a/solution.py
+++ b/solution.py
@@ -26,7 +26,7 @@
     scale, length, per,
     d_hbm, e_hbm, xt_ref, pick_ref, perm_ref,
     out_ref,
-    a, xt, e, m, d, lac, sq, wanted, kacc, gram, xtm, both, pn_ref,
+    a, xt, e, m, d, lac, sq, wanted, kacc, gram, xtm, both, terms, pn_ref,
     ring_send, ring_recv, sib_send, sib_recv, x_send, x_recv, xs_send, xs_recv, load_sem,
 ):
     half = length // 2
@@ -68,6 +68,25 @@
             device_id={"samp": sib}, device_id_type=MESH,
         )
 
+    small = chunk // 2
+
+    def half_span(q, part):
+        return pl.ds(pl.multiple_of(q * chunk + part * small, small), small)
+
+    def last_ring(q, n, target, part):
+        ref = a.at[2 * place(n) + core, half_span(q, part), :]
+        return pltpu.make_async_remote_copy(
+            src_ref=ref, dst_ref=ref, send_sem=ring_send.at[q, n if part == 0 else half + 1],
+            recv_sem=ring_recv.at[q, end + part], device_id={"samp": target}, device_id_type=MESH,
+        )
+
+    def last_across(q, part):
+        ref = a.at[2 * place(zero + end) + core, half_span(q, part), :]
+        return pltpu.make_async_remote_copy(
+            src_ref=ref, dst_ref=ref, send_sem=sib_send.at[q, end + part], recv_sem=sib_recv.at[q, end + part],
+            device_id={"samp": sib}, device_id_type=MESH,
+        )
+
     def x_ring(n, target, index, arrival):
         ref = xt.at[2 * place(n) + core]
         return pltpu.make_async_remote_copy(
@@ -88,36 +107,45 @@
     def own_x():
         return (x_ring(zero, up, 0, 1), x_ring(zero, down, half, 2), x_across(zero))
 
-    def comm(s, parity, link, cross, finish):
-        def arrive(n, target, forward):
+    def comm(s, parity, link, cross, finish, q=None):
+        def go(copy):
+            copy.wait_send() if finish else copy.start()
+
+        def arrive(n, target, mine):
             if not finish:
                 link(n, target, n, n).wait_recv()
-
-            @pl.when(forward)
-            def _():
-                copy = link(n, target, n, jnp.minimum(n + 2, end))
-                copy.wait_send() if finish else copy.start()
-
-            copy = cross(n)
-            copy.wait_send() if finish else copy.start()
+            whole = s < last - 1
+            tip = jnp.logical_and(s == last - 1, mine)
+
+            @pl.when(whole if q is not None else jnp.logical_or(whole, tip))
+            def _():
+                go(link(n, target, n, jnp.minimum(n + 2, end)))
+
+            if q is not None:
+                @pl.when(tip)
+                def _():
+                    for part in range(2):
+                        go(last_ring(q, n, target, part))
+
+            go(cross(n))
 
         @pl.when(s < last)
         def _():
-            arrive(2 * s - 1, up, jnp.logical_or(s < last - 1, parity == 0))
-            arrive(2 * s, down, jnp.logical_or(s < last - 1, parity == 1))
-
-        @pl.when(s == last)
-        def _():
-            if not finish:
-                link(end, up, end, end).wait_recv()
-            copy = cross(end)
-            copy.wait_send() if finish else copy.start()
+            arrive(2 * s - 1, up, parity == 0)
+            arrive(2 * s, down, parity == 1)
+
+        if q is None:
+            @pl.when(s == last)
+            def _():
+                if not finish:
+                    link(end, up, end, end).wait_recv()
+                go(cross(end))
 
     def chunk_comm(q, s, finish=False):
         comm(
             s, lax.rem(q, 2),
             lambda n, target, index, arrival: ring(q, n, target, index, arrival),
-            lambda n: across(q, n), finish,
+            lambda n: across(q, n), finish, q,
         )
 
     def x_comm(s, finish=False):
@@ -173,6 +201,8 @@
             m[lax.rem(n, ring_slots), mine, :] = dot(hot, e[...], (1, 0)).astype(BF16)
 
         loop(0, 2, part)
+
+    def measure(n):
         some = e[pl.ds(pl.multiple_of(n * pair, pair), pair), :].astype(F32)
         pn_ref[...] += jnp.sum(some * some, axis=0, keepdims=True)
 
@@ -180,32 +210,44 @@
         both = m[lax.rem(n, ring_slots)]
         return both[:rows], both[rows:]
 
-    def add(q, spots):
+    def collect(here, spots):
         blocks = []
         for n in spots:
-            across(q, n).wait_recv()
             at = 2 * place(n)
             mine = matched(n)
-            blocks += [(a[at + c, span(q), :], mine[c], xt[at + c]) for c in range(2)]
-        out_ref[span(q), :] += sum(dot(block, rest, (1, 0)) for block, rest, _ in blocks)
-        lac[q] += sum(dot(block, side, (1, 1)) for block, _, side in blocks)
+            blocks += [(a[at + c, here, :], mine[c], xt[at + c]) for c in range(2)]
+        out_ref[here, :] += sum(dot(block, rest, (1, 0)) for block, rest, _ in blocks)
+        lac[here, :covars] += sum(dot(block, side, (1, 1)) for block, _, side in blocks)
         total = sum(jnp.square(block.astype(F32)) for block, _, _ in blocks)
-        sq[q] += sum(total[:, c : c + sq.shape[2]] for c in range(0, rows, sq.shape[2]))
+        sq[here, :] += sum(total[:, c : c + sq.shape[1]] for c in range(0, rows, sq.shape[1]))
+
+    def add(q, spots):
+        for n in spots:
+            across(q, n).wait_recv()
+        collect(span(q), spots)
 
     def side(n):
         at = 2 * place(n)
         one, two = matched(n)
         xtm[...] += dot(xt[at], one, (1, 0)) + dot(xt[at + 1], two, (1, 0))
 
-    def finish_chunk(q):
-        loads = lac[q]
-        change = dot(loads, both[...], (1, 0), HIGHEST)
+    def split(x):
+        high = x.astype(BF16)
+        rest = x - high.astype(F32)
+        middle = rest.astype(BF16)
+        return high, middle, (rest - middle.astype(F32)).astype(BF16)
+
+    def finish(here):
+        loads = lac[here, :]
+        high, middle, low = split(loads)
+        one, two = jnp.concatenate([high, middle], axis=1), jnp.concatenate([high, low], axis=1)
+        change = dot(one, terms[0], (1, 0)) + (dot(one, terms[1], (1, 0)) + dot(two, terms[2], (1, 0)))
         genes = xtm.shape[1]
-        fitted, white = change[:, :genes], change[:, genes : genes + covars]
-        norm = jnp.sum(sq[q], axis=1, keepdims=True) + jnp.sum(white * loads, axis=1, keepdims=True)
+        fitted, white = change[:, :genes], change[:, genes:]
+        norm = jnp.sum(sq[here, :], axis=1, keepdims=True) + jnp.sum(white * loads, axis=1, keepdims=True)
         norm = jnp.maximum(norm, 0.0)
         row, column = scale * lax.rsqrt(norm + epsilon), lax.rsqrt(pn_ref[...] + epsilon)
-        out_ref[span(q), :] = (out_ref[span(q), :] + fitted) * row * column
+        out_ref[here, :] = (out_ref[here, :] + fitted) * row * column
 
     def sweep(k):
         whole = gram[...]
@@ -233,10 +275,10 @@
     for ref in (out_ref, lac, sq, gram, xtm, both, pn_ref):
         ref[...] = jnp.zeros(ref.shape, F32)
     load_e.wait()
-    loop(0, 2, permute)
+    permute(zero)
 
     ticks = CHUNKS * (last - 1)
-    per_tick = covars // 16
+    per_tick = covars // 8
 
     def tick(t):
         s = lax.div(t, CHUNKS) + 1
@@ -251,6 +293,10 @@
         def _():
             permute(2 * s + lax.div(j, 2))
 
+        @pl.when(t == 1)
+        def _():
+            permute(zero + 1)
+
         @pl.when(jnp.logical_and(j == 1, s == 1))
         def _():
             x_across(zero).wait_recv()
@@ -292,6 +338,8 @@
 
             loop(3, half, lambda n: x_across(n).wait_recv())
 
+        @pl.when(t == last + 1)
+        def _():
             def square(n):
                 at = 2 * place(n)
                 one, two = xt[at], xt[at + 1]
@@ -299,30 +347,53 @@
 
             loop(0, half, square)
 
-        @pl.when(jnp.logical_and(t > last, t <= last + 16))
-        def _():
-            loop((t - last - 1) * per_tick, (t - last) * per_tick, sweep)
+        odd = lax.rem(j, 2) == 1
+
+        @pl.when(odd)
+        def _():
+            measure(2 * s + lax.div(j, 2))
+
+        @pl.when(t == 3)
+        def _():
+            loop(0, 2, measure)
+
+        @pl.when(jnp.logical_and(odd, jnp.logical_and(t > last + 2, t < last + 18)))
+        def _():
+            turn = lax.div(t - last - 3, 2)
+            loop(turn * per_tick, (turn + 1) * per_tick, sweep)
 
     loop(0, ticks, tick)
 
     loop(end - 2, end + 1, side)
-    both[:, : xtm.shape[1]] = dot(gram[...], xtm[...], (1, 0), HIGHEST)
-    both[:, xtm.shape[1] : xtm.shape[1] + covars] = gram[...]
+    both[:covars, : xtm.shape[1]] = dot(gram[...], xtm[...], (1, 0), HIGHEST)
+    both[:covars, xtm.shape[1] : xtm.shape[1] + covars] = gram[...]
+    high, middle, low = split(both[...])
+    terms[0] = jnp.concatenate([high, high], axis=0)
+    terms[1] = jnp.concatenate([middle, middle], axis=0)
+    terms[2] = jnp.concatenate([low, high], axis=0)
     loop(0, CHUNKS, lambda q: add(q, (zero + end - 2, zero + end - 1)))
 
-    def closing(k):
-        first, final = 2 * k, 2 * k + 2
-        loop(first, final, lambda q: chunk_comm(q, zero + last))
-
-        def close(q):
-            add(q, (zero + end,))
-            finish_chunk(q)
-
-        loop(first, final, close)
-        loop(0, CHUNKS, lambda q: chunk_comm(q, last - 2 + k, True))
-
-    loop(0, CHUNKS // 2, closing)
-    loop(0, CHUNKS, lambda q: chunk_comm(q, zero + last, True))
+    for k in range(CHUNKS // 2):
+        for part in range(2):
+            def land(q):
+                copy = last_ring(q, zero + end, up, part)
+                copy.wait_recv()
+                last_across(q, part).start()
+
+            def close(q):
+                last_across(q, part).wait_recv()
+                collect(half_span(q, part), (zero + end,))
+                finish(half_span(q, part))
+
+            loop(2 * k, 2 * k + 2, land)
+            loop(2 * k, 2 * k + 2, close)
+        loop(0, CHUNKS, lambda q: chunk_comm(q, zero + last - 2 + k, True))
+
+    def retire(q):
+        for part in range(2):
+            last_across(q, part).wait_send()
+
+    loop(0, CHUNKS, retire)
 
 
 def local(length, dosage, covariates, expression, block_index, expr_row):
@@ -347,18 +418,19 @@
             pltpu.VMEM((samples, genes), BF16),
             pltpu.VMEM((8, 2 * rows, genes), BF16),
             pltpu.VMEM((rows, panel), BF16),
-            pltpu.VMEM((CHUNKS, chunk, covars), F32),
-            pltpu.VMEM((CHUNKS, chunk, min(rows, 128)), F32),
+            pltpu.VMEM((wide, 128), F32),
+            pltpu.VMEM((wide, 128), F32),
             pltpu.VMEM((2 * rows, 128), jnp.int32),
             pltpu.VMEM((rows, chunk), F32),
             pltpu.VMEM((covars, covars), F32),
             pltpu.VMEM((covars, genes), F32),
-            pltpu.VMEM((covars, genes + 128), F32),
+            pltpu.VMEM((128, genes + 128), F32),
+            pltpu.VMEM((3, 256, genes + 128), BF16),
             pltpu.VMEM((1, genes), F32),
+            dma((CHUNKS, half + 2)),
             dma((CHUNKS, half + 1)),
-            dma((CHUNKS, half)),
-            dma((CHUNKS, half)),
-            dma((CHUNKS, half)),
+            dma((CHUNKS, half + 1)),
+            dma((CHUNKS, half + 1)),
             dma((half + 1,)),
             dma((half,)),
             dma((half,)),

time: 212 us -> 214 us (level)
    pallas_call x1, Pallas kernels: 210 us -> 212 us  [local(): pl.pallas_call(lambda *refs: scan_kernel(scale, length, CHUNKS // blocks,...]
where the time goes in v3:
time: 214 us
  Pallas kernels  212 us (99%)
    pallas_call x1, Pallas kernels, local(): pl.pallas_call(lambda *refs: scan_kernel(scale, length, CHUNKS // blocks,...  212 us

profile of v3, /device:TPU:69, one launch (start us, length us, event | category | flops | bytes accessed | tf_op | source)
XLA Modules:
  0.0 213.8 jit_solution(16825192003152422639)
XLA Ops:
  0.0 211.8 %scan.1 = f32[2048,512]{1,0:T(8,128)S(1)} custom-call(bf16[256,8192]{1,0:T(8,128)(2,1)} %refs_0_.1, bf16[8192,512]{1,0:T(8,128)(2,1)} %refs_1_.1, bf16[96,256]{1,0:T(8,128)(2,1)} %bitcast.2, s32[2,1024]{1,0:T(2,128)} %refs_3_.1, s32[1,8192]{1,0:T(1,128)} %bitcast.3), custom_call_target="tpu_custom_call" | custom-call | tf_op jit(solution)/shard_map/scan/pallas_call | solution.py:410
  211.8 2.0 copy.7
